TPU v7x, 32 devices: a whole 2x2x4 slice. The times are simulated.
32 devices in a mesh: tile: 16 (over z, y, x), lev: 2 (over core).
Axes of the slice: x: 2, y: 2, z: 4, core: 2. Of those that a mesh axis runs over, the one named last changes fastest.
Arguments:
- increments: bfloat16 [136, 256, 1024], P('lev', 'tile'), may hold values from -30 to 30
- projection: bfloat16 [80, 136], replicated, may hold values from -0.5 to 0.5
- helmholtz: float32 [80], P('lev'), may hold values from 0.05 to 4
Outputs:
- solution: float32 [80, 256, 1024], P('lev', 'tile')
- residual: float32 [80, 256, 1024], P('lev', 'tile')
All inputs are finite; a program needn't handle non-finite values.
Results may differ from a plain program's by a relative error of at most 0.00075.
Values may be sent and summed in bfloat16 or wider, within the bound.
A program may use at most 192 MiB of HBM per device.

v0:
```python
import jax
import jax.numpy as jnp
import numpy as np
from jax import lax
from jax.sharding import PartitionSpec as P

S = 4
BLOCKS = 2
highest = lax.Precision.HIGHEST


def extended(block, sides, width):
    for axis, dim in sides:
        count = lax.axis_size(axis)
        forward = [(i, i + 1) for i in range(count - 1)]
        backward = [(target, source) for source, target in forward]
        low = lax.ppermute(
            lax.slice_in_dim(block, block.shape[dim] - width, None, axis=dim), axis, forward
        )
        high = lax.ppermute(lax.slice_in_dim(block, 0, width, axis=dim), axis, backward)
        block = jnp.concatenate([low, block, high], axis=dim)
    return block


def shift_matrix():
    width = 2 * S + 1
    table = np.zeros((width, width), np.float32)
    for index in range(S):
        table[index + 1, index] = 1.0
    for index in range(S - 1):
        table[S + 2 + index, S + 1 + index] = 1.0
    return jnp.asarray(table, jnp.float32)


def stencil_rows(field, weight_col):
    padded = extended(field, (("tile", 1),), 1)
    side = jnp.pad(field, ((0, 0), (0, 0), (1, 1)))
    beside_all = padded[:, 2:, :] + padded[:, :-2, :] + side[:, :, 2:] + side[:, :, :-2]
    return weight_col * beside_all


def quadratic(gram, left, right):
    return jnp.einsum("ma,mab,mb->m", left, gram, right, precision=highest)


def combine(coef, vectors):
    total = coef[:, 0, None, None] * vectors[0]
    for index in range(1, len(vectors)):
        total = total + coef[:, index, None, None] * vectors[index]
    return total


def inner_table(vectors):
    width = len(vectors)
    cached = {}
    for first in range(width):
        for second in range(first, width):
            cached[first, second] = jnp.sum(vectors[first] * vectors[second], axis=(1, 2))
    rows_list = []
    for first in range(width):
        entries = []
        for second in range(width):
            entries.append(cached[min(first, second), max(first, second)])
        rows_list.append(jnp.stack(entries, axis=1))
    return jnp.stack(rows_list, axis=1)


def shards(increments, projection, helmholtz):
    lev_count, rows_x, cells_y = increments.shape
    mode_count = projection.shape[0] // lax.axis_size("lev")
    flat = increments.reshape(lev_count, rows_x * cells_y)
    own_cols = lax.dynamic_slice_in_dim(projection, lax.axis_index("lev") * lev_count, lev_count, 1)
    modal = lax.psum_scatter(
        jnp.dot(own_cols, flat, preferred_element_type=jnp.float32),
        "lev",
        scatter_dimension=0,
        tiled=True,
    )
    modal = modal.reshape(mode_count, rows_x, cells_y)
    weight_col = (1.0 / (4.0 + helmholtz))[:, None, None]
    width = 2 * S + 1
    shifter = shift_matrix()
    solution = jnp.zeros_like(modal)
    resid = modal
    direction = modal
    for block_index in range(BLOCKS):
        vectors = [direction]
        current = direction
        for power_index in range(S):
            current = stencil_rows(current, weight_col)
            vectors.append(current)
        vectors.append(resid)
        current = resid
        for power_index in range(S - 1):
            current = stencil_rows(current, weight_col)
            vectors.append(current)
        gram = inner_table(vectors)
        gram = lax.psum(gram, "tile")
        p_coef = jnp.zeros((mode_count, width), jnp.float32).at[:, 0].set(1.0)
        r_coef = jnp.zeros((mode_count, width), jnp.float32).at[:, S + 1].set(1.0)
        x_coef = jnp.zeros((mode_count, width), jnp.float32)
        squares = quadratic(gram, r_coef, r_coef)
        for step_index in range(S):
            moved = p_coef - jnp.einsum("ab,mb->ma", shifter, p_coef, precision=highest)
            alpha = (squares / quadratic(gram, p_coef, moved))[:, None]
            x_coef = x_coef + alpha * p_coef
            r_coef = r_coef - alpha * moved
            fresh = quadratic(gram, r_coef, r_coef)
            p_coef = r_coef + (fresh / squares)[:, None] * p_coef
            squares = fresh
        solution = solution + combine(x_coef, vectors)
        resid = combine(r_coef, vectors)
        direction = combine(p_coef, vectors)
    return (solution, resid)


def solution(mesh):
    in_specs = (P("lev", "tile", None), P(), P("lev"))
    out_specs = (P("lev", "tile", None), P("lev", "tile", None))
    return jax.shard_map(shards, mesh=mesh, in_specs=in_specs, out_specs=out_specs, check_vma=False)
```

profile of v0, /device:TPU:0, one launch (start us, length us, event | category | flops | bytes accessed | tf_op | source)
XLA Modules:
  0.0 469.2 jit_solution(7739262353369601456)
XLA Ops:
  12.1 4.9 %fusion.44 = f32[80,16384]{1,0:T(8,128)} fusion(bf16[68,16384]{1,0:T(8,128)(2,1)} %bitcast.230, bf16[80,136]{0,1:T(8,128)(2,1)S(1)} %copy-done, s32[]{:T(128)S(6)} %select_n.3), kind=kOutput, calls=%fused_computation.212 | convolution fusion | flops 178257920 | bytes 7489540 | tf_op jit(solution)/shard_map/dot_general | solution.py:74
  17.0 15.9 %reduce-scatter.2.cloned.1.call-done = f32[40,16384]{1,0:T(8,128)} async-done(((f32[80,16384]{1,0:T(8,128)}), f32[40,16384]{1,0:T(8,128)}) %reduce-scatter.2.cloned.1.call-update) | async-done | bytes 2621456 | tf_op jit(solution)/shard_map/reduce_scatter | solution.py:73
  36.3 4.6 collective-permute-start.1
  52.1 5.0 %collective-permute-start.3 = (f32[40,1,1024]{2,0,1:T(8,128)S(1)}, f32[40,1,1024]{2,0,1:T(8,128)S(1)}, u32[]{:S(2)}, u32[]{:S(2)}) collective-permute-start(f32[40,1,1024]{2,0,1:T(8,128)S(1)} %get-tuple-element.129), channel_id=1, source_target_pairs={{0,2},{2,4},{4,6},{6,8},{8,10},{10,12},{12,14},{14,16},{16,18},{18... | collective-permute-start | bytes 491528 | tf_op jit(solution)/shard_map/ppermute | solution.py:17
  61.8 5.6 %fusion.5 = f32[40,16,1024]{2,0,1:T(8,128)S(1)} fusion(f32[40,16,1024]{2,0,1:T(8,128)} %copy-done.18, f32[40,1,1024]{2,0,1:T(8,128)S(1)} %collective-permute-done.3, f32[40,1,1024]{2,0,1:T(8,128)S(1)} %collective-permute-done.2, f32[40]{0:T(128)S(1)} %add_divide_fusion), kind=kLoop, calls=%fused_computation.27 | loop fusion | flops 3932160 | bytes 5570720 | tf_op jit(solution)/shard_map/mul | solution.py:39
  69.6 5.0 %collective-permute-start.5 = (f32[40,1,1024]{2,0,1:T(8,128)}, f32[40,1,1024]{2,0,1:T(8,128)S(1)}, u32[]{:S(2)}, u32[]{:S(2)}) collective-permute-start(f32[40,1,1024]{2,0,1:T(8,128)} %get-tuple-element.127), channel_id=1, source_target_pairs={{0,2},{2,4},{4,6},{6,8},{8,10},{10,12},{12,14},{14,16},{16,18},{18... | collective-permute-start | bytes 491528 | tf_op jit(solution)/shard_map/ppermute | solution.py:17
  81.8 5.5 %fusion.8 = f32[40,16,1024]{2,0,1:T(8,128)S(1)} fusion(f32[40,16,1024]{2,0,1:T(8,128)} %copy-done.6, f32[40,1,1024]{2,0,1:T(8,128)S(1)} %collective-permute-done.5, f32[40,1,1024]{2,0,1:T(8,128)S(1)} %collective-permute-done.4, f32[40]{0:T(128)S(1)} %add_divide_fusion), kind=kLoop, calls=%fused_computation.30 | loop fusion | flops 3932160 | bytes 5570720 | tf_op jit(solution)/shard_map/mul | solution.py:39
  88.9 4.9 %collective-permute-start.7 = (f32[40,1,1024]{2,0,1:T(8,128)S(1)}, f32[40,1,1024]{2,0,1:T(8,128)S(1)}, u32[]{:S(2)}, u32[]{:S(2)}) collective-permute-start(f32[40,1,1024]{2,0,1:T(8,128)S(1)} %get-tuple-element.125), channel_id=1, source_target_pairs={{0,2},{2,4},{4,6},{6,8},{8,10},{10,12},{12,14},{14,16},{16,18},{18... | collective-permute-start | bytes 491528 | tf_op jit(solution)/shard_map/ppermute | solution.py:17
  98.5 5.4 %multiply_reduce_fusion.45 = (f32[40]{0:T(128)S(1)}, f32[40]{0:T(128)S(1)}, f32[40]{0:T(128)S(1)}, f32[40]{0:T(128)S(1)}, f32[40]{0:T(128)S(1)}, /*index=5*/f32[...) fusion(f32[40,16,1024]{2,0,1:T(8,128)S(1)} %fusion.8, ...), kind=kLoop, calls=%fused_computation.138 | loop fusion | flops 26213840 | bytes 11143520 | tf_op jit(solution)/shard_map/reduce_sum | solution.py:58
  104.2 75.3 %psum.14 = f32[40,9,9]{0,2,1:T(8,128)S(1)} all-reduce(f32[40,9,9]{0,2,1:T(8,128)S(1)} %constant_dynamic-update-slice_fusion), channel_id=1, replica_groups=mesh['tile'=16,'lev'=2] {'tile'}, use_global_device_ids=true, to_apply=%region_17.18 | all-reduce | flops 3240 | bytes 25920 | tf_op jit(solution)/shard_map/psum | solution.py:98
  183.8 13.6 %multiply_add_fusion.2 = f32[40,16,1024]{2,0,1:T(8,128)S(1)} fusion(f32[40,16,1024]{2,0,1:T(8,128)} %copy-done.6, f32[40,16,1024]{2,0,1:T(8,128)} %get-tuple-element.109, f32[40]{0:T(128)S(1)} %get-tuple-element.162, f32[40]{0:T(128)S(1)} %get-tuple-element.163, f32[40]{0:T(128)S(1)} %get-tuple-element.164, f32[40]{0:T(128)S(1)} %get-tuple-element.165, ...), kind=kLoop, calls=%fused_computation.137 | loop fusion | flops 19005440 | bytes 13764160 | tf_op jit(solution)/shard_map/add | solution.py:49
  198.7 4.6 collective-permute-start.9
  203.3 5.8 %multiply_add_fusion.1 = f32[40,16,1024]{2,0,1:T(8,128)S(1)} fusion(f32[40,16,1024]{2,0,1:T(8,128)S(1)} %copy-done.7, f32[40,16,1024]{2,0,1:T(8,128)S(1)} %copy-done.17, f32[40]{0:T(128)S(1)} %get-tuple-element.171, f32[40]{0:T(128)S(1)} %get-tuple-element.172, f32[40]{0:T(128)S(1)} %get-tuple-element.173, f32[40]{0:T(128)S(1)} %get-tuple-element.174, ...), kind=kLoop, calls=%fused_computation.131 | loop fusion | flops 19005440 | bytes 13764160 | tf_op jit(solution)/shard_map/add | solution.py:49
  211.9 4.6 collective-permute-start.11
  217.8 4.6 collective-permute-start.17
  225.2 5.0 %collective-permute-start.13 = (f32[40,1,1024]{2,0,1:T(8,128)S(1)}, f32[40,1,1024]{2,0,1:T(8,128)S(1)}, u32[]{:S(2)}, u32[]{:S(2)}) collective-permute-start(f32[40,1,1024]{2,0,1:T(8,128)S(1)} %get-tuple-element.115), channel_id=1, source_target_pairs={{0,2},{2,4},{4,6},{6,8},{8,10},{10,12},{12,14},{14,16},{16,18},{18... | collective-permute-start | bytes 491528 | tf_op jit(solution)/shard_map/ppermute | solution.py:17
  239.2 6.9 %collective-permute-start.19 = (f32[40,1,1024]{2,0,1:T(8,128)S(1)}, f32[40,1,1024]{2,0,1:T(8,128)S(1)}, u32[]{:S(2)}, u32[]{:S(2)}) collective-permute-start(f32[40,1,1024]{2,0,1:T(8,128)S(1)} %get-tuple-element.121), channel_id=1, source_target_pairs={{0,2},{2,4},{4,6},{6,8},{8,10},{10,12},{12,14},{14,16},{16,18},{18... | collective-permute-start | bytes 491528 | tf_op jit(solution)/shard_map/ppermute | solution.py:17
  247.4 6.1 %collective-permute-start.15 = (f32[40,1,1024]{2,0,1:T(8,128)S(1)}, f32[40,1,1024]{2,0,1:T(8,128)}, u32[]{:S(2)}, u32[]{:S(2)}) collective-permute-start(f32[40,1,1024]{2,0,1:T(8,128)S(1)} %get-tuple-element.113), channel_id=1, source_target_pairs={{0,2},{2,4},{4,6},{6,8},{8,10},{10,12},{12,14},{14,16},{16,18},{18... | collective-permute-start | bytes 491528 | tf_op jit(solution)/shard_map/ppermute | solution.py:17
  257.8 5.7 %collective-permute-start.21 = (f32[40,1,1024]{2,0,1:T(8,128)S(1)}, f32[40,1,1024]{2,0,1:T(8,128)}, u32[]{:S(2)}, u32[]{:S(2)}) collective-permute-start(f32[40,1,1024]{2,0,1:T(8,128)S(1)} %get-tuple-element.111), channel_id=1, source_target_pairs={{0,2},{2,4},{4,6},{6,8},{8,10},{10,12},{12,14},{14,16},{16,18},{18... | collective-permute-start | bytes 491528 | tf_op jit(solution)/shard_map/ppermute | solution.py:17
  265.7 24.5 %multiply_reduce_fusion = (f32[40]{0:T(128)}, f32[40]{0:T(128)}, f32[40]{0:T(128)}, f32[40]{0:T(128)}, f32[40]{0:T(128)}, /*index=5*/f32[40]{0:T(128)}, f32[40]{...) fusion(f32[40,16,1024]{2,0,1:T(8,128)} %copy-done.20, ...), kind=kLoop, calls=%fused_computation.91 | loop fusion | flops 70777080 | bytes 21961920 | tf_op jit(solution)/shard_map/reduce_sum | solution.py:58
  308.2 77.3 %psum.15 = f32[40,9,9]{0,2,1:T(8,128)S(1)} all-reduce(f32[40,9,9]{0,2,1:T(8,128)} %constant_dynamic-update-slice_fusion.9), channel_id=1, replica_groups=mesh['tile'=16,'lev'=2] {'tile'}, use_global_device_ids=true, to_apply=%region_64.65 | all-reduce | flops 3240 | bytes 25920 | tf_op jit(solution)/shard_map/psum | solution.py:98
  422.2 19.2 %multiply_add_fusion = f32[40,16,1024]{2,0,1:T(8,128)} fusion(f32[40,16,1024]{2,0,1:T(8,128)} %get-tuple-element.108, f32[40,16,1024]{2,0,1:T(8,128)} %copy-done.15, f32[40,16,1024]{2,0,1:T(8,128)} %copy-done.11, f32[40,16,1024]{2,0,1:T(8,128)} %get-tuple-element.107, f32[40,16,1024]{2,0,1:T(8,128)} %copy-done.16, f32[40,16,1024]{2,0,1:T(8,128)} %copy-done.13, ...), kind=kLoop, calls=%fused_computation.89 | loop fusion | flops 19005440 | bytes 21628480 | tf_op jit(solution)/shard_map/add | solution.py:49
  441.5 4.9 %copy.22 = f32[40,16,1024]{2,1,0:T(8,128)} copy(f32[40,16,1024]{2,0,1:T(8,128)} %multiply_add_fusion) | data formatting | bytes 5242880
  446.5 12.8 %add_add_fusion = f32[40,16,1024]{2,0,1:T(8,128)S(1)} fusion(f32[40,16,1024]{2,0,1:T(8,128)} %get-tuple-element.108, f32[40,16,1024]{2,0,1:T(8,128)} %copy-done.15, f32[40,16,1024]{2,0,1:T(8,128)S(1)} %copy-done.12, f32[40,16,1024]{2,0,1:T(8,128)} %get-tuple-element.107, f32[40,16,1024]{2,0,1:T(8,128)} %copy-done.16, f32[40,16,1024]{2,0,1:T(8,128)S(1)} %copy-done.14, ...), kind=kLoop, calls=%fused_computation.90 | loop fusion | flops 38666240 | bytes 32771040 | tf_op jit(solution)/shard_map/add | solution.py:111
  (343 shorter events, 124.9 us)
Async XLA Ops:
  7.2 25.7 %reduce-scatter.2.cloned.1.call-start = ((), (), s32[]{:S(2)}) async-start(), calls=%async_computation.1 | async-start | bytes 7864320 | tf_op jit(solution)/shard_map/reduce_scatter | solution.py:73
  35.0 8.3 %collective-permute-start = (f32[40,1,1024]{2,0,1:T(8,128)S(1)}, f32[40,1,1024]{2,0,1:T(8,128)S(1)}, u32[]{:S(2)}, u32[]{:S(2)}) collective-permute-start(f32[40,1,1024]{2,0,1:T(8,128)S(1)} %get-tuple-element.130), channel_id=1, source_target_pairs={{2,0},{4,2},{6,4},{8,6},{10,8},{12,10},{14,12},{16,14},{18,16},{20... | collective-permute-start | bytes 491528 | tf_op jit(solution)/shard_map/ppermute | solution.py:20
  36.3 11.5 %collective-permute-start.1 = (f32[40,1,1024]{2,0,1:T(8,128)S(1)}, f32[40,1,1024]{2,0,1:T(8,128)S(1)}, u32[]{:S(2)}, u32[]{:S(2)}) collective-permute-start(f32[40,1,1024]{2,0,1:T(8,128)S(1)} %get-tuple-element.131), channel_id=1, source_target_pairs={{0,2},{2,4},{4,6},{6,8},{8,10},{10,12},{12,14},{14,16},{16,18},{18... | collective-permute-start | bytes 491528 | tf_op jit(solution)/shard_map/ppermute | solution.py:17
  40.9 142.9 %copy-start.35 = (f32[40]{0:T(128)}, f32[40]{0:T(128)S(1)}, u32[]{:S(2)}) copy-start(f32[40]{0:T(128)S(1)} %add_divide_fusion) | copy-start | bytes 484
  50.8 9.1 %collective-permute-start.2 = (f32[40,1,1024]{2,0,1:T(8,128)}, f32[40,1,1024]{2,0,1:T(8,128)S(1)}, u32[]{:S(2)}, u32[]{:S(2)}) collective-permute-start(f32[40,1,1024]{2,0,1:T(8,128)} %get-tuple-element.128), channel_id=1, source_target_pairs={{2,0},{4,2},{6,4},{8,6},{10,8},{12,10},{14,12},{16,14},{18,16},{20... | collective-permute-start | bytes 491528 | tf_op jit(solution)/shard_map/ppermute | solution.py:20
  52.1 9.7 %collective-permute-start.3 = (f32[40,1,1024]{2,0,1:T(8,128)S(1)}, f32[40,1,1024]{2,0,1:T(8,128)S(1)}, u32[]{:S(2)}, u32[]{:S(2)}) collective-permute-start(f32[40,1,1024]{2,0,1:T(8,128)S(1)} %get-tuple-element.129), channel_id=1, source_target_pairs={{0,2},{2,4},{4,6},{6,8},{8,10},{10,12},{12,14},{14,16},{16,18},{18... | collective-permute-start | bytes 491528 | tf_op jit(solution)/shard_map/ppermute | solution.py:17
  68.3 9.0 %collective-permute-start.4 = (f32[40,1,1024]{2,0,1:T(8,128)}, f32[40,1,1024]{2,0,1:T(8,128)S(1)}, u32[]{:S(2)}, u32[]{:S(2)}) collective-permute-start(f32[40,1,1024]{2,0,1:T(8,128)} %get-tuple-element.126), channel_id=1, source_target_pairs={{2,0},{4,2},{6,4},{8,6},{10,8},{12,10},{14,12},{16,14},{18,16},{20... | collective-permute-start | bytes 491528 | tf_op jit(solution)/shard_map/ppermute | solution.py:20
  69.6 12.2 %collective-permute-start.5 = (f32[40,1,1024]{2,0,1:T(8,128)}, f32[40,1,1024]{2,0,1:T(8,128)S(1)}, u32[]{:S(2)}, u32[]{:S(2)}) collective-permute-start(f32[40,1,1024]{2,0,1:T(8,128)} %get-tuple-element.127), channel_id=1, source_target_pairs={{0,2},{2,4},{4,6},{6,8},{8,10},{10,12},{12,14},{14,16},{16,18},{18... | collective-permute-start | bytes 491528 | tf_op jit(solution)/shard_map/ppermute | solution.py:17
  87.4 8.9 %collective-permute-start.6 = (f32[40,1,1024]{2,0,1:T(8,128)S(1)}, f32[40,1,1024]{2,0,1:T(8,128)S(1)}, u32[]{:S(2)}, u32[]{:S(2)}) collective-permute-start(f32[40,1,1024]{2,0,1:T(8,128)S(1)} %get-tuple-element.124), channel_id=1, source_target_pairs={{2,0},{4,2},{6,4},{8,6},{10,8},{12,10},{14,12},{16,14},{18,16},{20... | collective-permute-start | bytes 491528 | tf_op jit(solution)/shard_map/ppermute | solution.py:20
  88.9 9.6 %collective-permute-start.7 = (f32[40,1,1024]{2,0,1:T(8,128)S(1)}, f32[40,1,1024]{2,0,1:T(8,128)S(1)}, u32[]{:S(2)}, u32[]{:S(2)}) collective-permute-start(f32[40,1,1024]{2,0,1:T(8,128)S(1)} %get-tuple-element.125), channel_id=1, source_target_pairs={{0,2},{2,4},{4,6},{6,8},{8,10},{10,12},{12,14},{14,16},{16,18},{18... | collective-permute-start | bytes 491528 | tf_op jit(solution)/shard_map/ppermute | solution.py:17
  197.4 11.7 %collective-permute-start.8 = (f32[40,1,1024]{2,0,1:T(8,128)S(1)}, f32[40,1,1024]{2,0,1:T(8,128)S(1)}, u32[]{:S(2)}, u32[]{:S(2)}) collective-permute-start(f32[40,1,1024]{2,0,1:T(8,128)S(1)} %get-tuple-element.118), channel_id=1, source_target_pairs={{2,0},{4,2},{6,4},{8,6},{10,8},{12,10},{14,12},{16,14},{18,16},{20... | collective-permute-start | bytes 491528 | tf_op jit(solution)/shard_map/ppermute | solution.py:20
  198.7 10.4 %collective-permute-start.9 = (f32[40,1,1024]{2,0,1:T(8,128)S(1)}, f32[40,1,1024]{2,0,1:T(8,128)S(1)}, u32[]{:S(2)}, u32[]{:S(2)}) collective-permute-start(f32[40,1,1024]{2,0,1:T(8,128)S(1)} %get-tuple-element.119), channel_id=1, source_target_pairs={{0,2},{2,4},{4,6},{6,8},{8,10},{10,12},{12,14},{14,16},{16,18},{18... | collective-permute-start | bytes 491528 | tf_op jit(solution)/shard_map/ppermute | solution.py:17
  210.6 11.8 %collective-permute-start.10 = (f32[40,1,1024]{2,0,1:T(8,128)S(1)}, f32[40,1,1024]{2,0,1:T(8,128)S(1)}, u32[]{:S(2)}, u32[]{:S(2)}) collective-permute-start(f32[40,1,1024]{2,0,1:T(8,128)S(1)} %get-tuple-element.116), channel_id=1, source_target_pairs={{2,0},{4,2},{6,4},{8,6},{10,8},{12,10},{14,12},{16,14},{18,16},{20... | collective-permute-start | bytes 491528 | tf_op jit(solution)/shard_map/ppermute | solution.py:20
  211.9 10.5 %collective-permute-start.11 = (f32[40,1,1024]{2,0,1:T(8,128)S(1)}, f32[40,1,1024]{2,0,1:T(8,128)S(1)}, u32[]{:S(2)}, u32[]{:S(2)}) collective-permute-start(f32[40,1,1024]{2,0,1:T(8,128)S(1)} %get-tuple-element.117), channel_id=1, source_target_pairs={{0,2},{2,4},{4,6},{6,8},{8,10},{10,12},{12,14},{14,16},{16,18},{18... | collective-permute-start | bytes 491528 | tf_op jit(solution)/shard_map/ppermute | solution.py:17
  216.5 13.7 %collective-permute-start.16 = (f32[40,1,1024]{2,0,1:T(8,128)S(1)}, f32[40,1,1024]{2,0,1:T(8,128)S(1)}, u32[]{:S(2)}, u32[]{:S(2)}) collective-permute-start(f32[40,1,1024]{2,0,1:T(8,128)S(1)} %get-tuple-element.122), channel_id=1, source_target_pairs={{2,0},{4,2},{6,4},{8,6},{10,8},{12,10},{14,12},{16,14},{18,16},{20... | collective-permute-start | bytes 491528 | tf_op jit(solution)/shard_map/ppermute | solution.py:20
  217.8 12.4 %collective-permute-start.17 = (f32[40,1,1024]{2,0,1:T(8,128)S(1)}, f32[40,1,1024]{2,0,1:T(8,128)S(1)}, u32[]{:S(2)}, u32[]{:S(2)}) collective-permute-start(f32[40,1,1024]{2,0,1:T(8,128)S(1)} %get-tuple-element.123), channel_id=1, source_target_pairs={{0,2},{2,4},{4,6},{6,8},{8,10},{10,12},{12,14},{14,16},{16,18},{18... | collective-permute-start | bytes 491528 | tf_op jit(solution)/shard_map/ppermute | solution.py:17
  223.9 8.7 %collective-permute-start.12 = (f32[40,1,1024]{2,0,1:T(8,128)S(1)}, f32[40,1,1024]{2,0,1:T(8,128)S(1)}, u32[]{:S(2)}, u32[]{:S(2)}) collective-permute-start(f32[40,1,1024]{2,0,1:T(8,128)S(1)} %get-tuple-element.114), channel_id=1, source_target_pairs={{2,0},{4,2},{6,4},{8,6},{10,8},{12,10},{14,12},{16,14},{18,16},{20... | collective-permute-start | bytes 491528 | tf_op jit(solution)/shard_map/ppermute | solution.py:20
  225.2 9.3 %collective-permute-start.13 = (f32[40,1,1024]{2,0,1:T(8,128)S(1)}, f32[40,1,1024]{2,0,1:T(8,128)S(1)}, u32[]{:S(2)}, u32[]{:S(2)}) collective-permute-start(f32[40,1,1024]{2,0,1:T(8,128)S(1)} %get-tuple-element.115), channel_id=1, source_target_pairs={{0,2},{2,4},{4,6},{6,8},{8,10},{10,12},{12,14},{14,16},{16,18},{18... | collective-permute-start | bytes 491528 | tf_op jit(solution)/shard_map/ppermute | solution.py:17
  237.9 15.7 %collective-permute-start.18 = (f32[40,1,1024]{2,0,1:T(8,128)S(1)}, f32[40,1,1024]{2,0,1:T(8,128)S(1)}, u32[]{:S(2)}, u32[]{:S(2)}) collective-permute-start(f32[40,1,1024]{2,0,1:T(8,128)S(1)} %get-tuple-element.120), channel_id=1, source_target_pairs={{2,0},{4,2},{6,4},{8,6},{10,8},{12,10},{14,12},{16,14},{18,16},{20... | collective-permute-start | bytes 491528 | tf_op jit(solution)/shard_map/ppermute | solution.py:20
  239.2 14.4 %collective-permute-start.19 = (f32[40,1,1024]{2,0,1:T(8,128)S(1)}, f32[40,1,1024]{2,0,1:T(8,128)S(1)}, u32[]{:S(2)}, u32[]{:S(2)}) collective-permute-start(f32[40,1,1024]{2,0,1:T(8,128)S(1)} %get-tuple-element.121), channel_id=1, source_target_pairs={{0,2},{2,4},{4,6},{6,8},{8,10},{10,12},{12,14},{14,16},{16,18},{18... | collective-permute-start | bytes 491528 | tf_op jit(solution)/shard_map/ppermute | solution.py:17
  246.1 18.0 %collective-permute-start.14 = (f32[40,1,1024]{2,0,1:T(8,128)S(1)}, f32[40,1,1024]{2,0,1:T(8,128)}, u32[]{:S(2)}, u32[]{:S(2)}) collective-permute-start(f32[40,1,1024]{2,0,1:T(8,128)S(1)} %get-tuple-element.112), channel_id=1, source_target_pairs={{2,0},{4,2},{6,4},{8,6},{10,8},{12,10},{14,12},{16,14},{18,16},{20... | collective-permute-start | bytes 491528 | tf_op jit(solution)/shard_map/ppermute | solution.py:20
  247.4 16.7 %collective-permute-start.15 = (f32[40,1,1024]{2,0,1:T(8,128)S(1)}, f32[40,1,1024]{2,0,1:T(8,128)}, u32[]{:S(2)}, u32[]{:S(2)}) collective-permute-start(f32[40,1,1024]{2,0,1:T(8,128)S(1)} %get-tuple-element.113), channel_id=1, source_target_pairs={{0,2},{2,4},{4,6},{6,8},{8,10},{10,12},{12,14},{14,16},{16,18},{18... | collective-permute-start | bytes 491528 | tf_op jit(solution)/shard_map/ppermute | solution.py:17
  256.5 7.8 %collective-permute-start.20 = (f32[40,1,1024]{2,0,1:T(8,128)S(1)}, f32[40,1,1024]{2,0,1:T(8,128)}, u32[]{:S(2)}, u32[]{:S(2)}) collective-permute-start(f32[40,1,1024]{2,0,1:T(8,128)S(1)} %get-tuple-element.110), channel_id=1, source_target_pairs={{2,0},{4,2},{6,4},{8,6},{10,8},{12,10},{14,12},{16,14},{18,16},{20... | collective-permute-start | bytes 491528 | tf_op jit(solution)/shard_map/ppermute | solution.py:20
  257.8 7.9 %collective-permute-start.21 = (f32[40,1,1024]{2,0,1:T(8,128)S(1)}, f32[40,1,1024]{2,0,1:T(8,128)}, u32[]{:S(2)}, u32[]{:S(2)}) collective-permute-start(f32[40,1,1024]{2,0,1:T(8,128)S(1)} %get-tuple-element.111), channel_id=1, source_target_pairs={{0,2},{2,4},{4,6},{6,8},{8,10},{10,12},{12,14},{14,16},{16,18},{18... | collective-permute-start | bytes 491528 | tf_op jit(solution)/shard_map/ppermute | solution.py:17
  (72 other events, 1497.5 us)
Sparse Core Ops, SparseCore 0:
  17.1 15.7 reduce-scatter.1
where the time goes:
time: 471 us; the launch traced here: 469 us
  blocking collectives  153 us (32%)
  other arithmetic  124 us (26%)
  starting transfers between devices  71.4 us (15%)
  local copies, waits for them, and re-layouts  55.5 us (12%)
  waiting for transfers between devices  41.9 us (9%)
  between operations  16.7 us (4%)
  matrix products  7.1 us (2%)
    psum x2, blocking collectives, shards(): gram = lax.psum(gram, 'tile')  153 us
    ppermute x11, starting transfers between devices, extended(): lax.ppermute(lax.slice_in_dim(block, block.shape[dim] - width, None, axis...  56.9 us
    add x3, other arithmetic, combine(): total = total + coef[:, index, None, None] * vectors[index]  38.5 us
    reduce_sum x3, other arithmetic, inner_table(): jnp.sum(vectors[first] * vectors[second], axis=(1, 2))  30.2 us
    unnamed x180, local copies, waits for them, and re-layouts  29.2 us
    mul x7, other arithmetic, stencil_rows(): return weight_col * beside_all  20.1 us
    ppermute x11, waiting for transfers between devices, extended(): lax.ppermute(lax.slice_in_dim(block, block.shape[dim] - width, None, axis...  16.6 us
    reduce_scatter x1, waiting for transfers between devices, shards(): lax.psum_scatter(jnp.dot(own_cols, flat, preferred_element_type=jnp.float...  15.9 us
  transfers between devices with their start and end apart: 23, of which 12 were waited for; matrix products, arithmetic and copies ran while one was open for 2% of the time, Pallas kernels for 0%

commit v1 on v0

--- a/solution.py
+++ b/solution.py
@@ -95,7 +95,14 @@
             current = stencil_rows(current, weight_col)
             vectors.append(current)
         gram = inner_table(vectors)
-        gram = lax.psum(gram, "tile")
+        count_2 = lax.axis_size("tile")
+        result, far = (gram, 1)
+        while far < count_2:
+            result = result + lax.ppermute(
+                result, "tile", [(i_2, i_2 ^ far) for i_2 in range(count_2)]
+            )
+            far = 2 * far
+        gram = result
         p_coef = jnp.zeros((mode_count, width), jnp.float32).at[:, 0].set(1.0)
         r_coef = jnp.zeros((mode_count, width), jnp.float32).at[:, S + 1].set(1.0)
         x_coef = jnp.zeros((mode_count, width), jnp.float32)

time: 471 us -> 352 us (0.75)
  blocking collectives: 153 us -> 0 us
  starting transfers between devices: 71.4 us -> 102 us
  waiting for transfers between devices: 41.9 us -> 58.6 us
  other arithmetic: 124 us -> 117 us
  local copies, waits for them, and re-layouts: 55.5 us -> 49 us
    psum x2 -> x0, blocking collectives: 153 us -> none  [shards(): gram = lax.psum(gram, 'tile')]
    ppermute x0 -> x8, starting transfers between devices: none -> 29.4 us  [shards(): lax.ppermute(result, 'tile', [(i_2, i_2 ^ far) for i_2 in range(count_2)])]
    ppermute x0 -> x8, waiting for transfers between devices: none -> 14.6 us  [shards(): lax.ppermute(result, 'tile', [(i_2, i_2 ^ far) for i_2 in range(count_2)])]
    mul x7, other arithmetic: 20.1 us -> 11.8 us  [stencil_rows(): return weight_col * beside_all]
    unnamed x180 -> x162, local copies, waits for them, and re-layouts: 29.2 us -> 23.1 us
  transfers between devices with their start and end apart: 23 -> 31, of which waited for: 12 -> 22; matrix products, arithmetic and copies ran while one was open for 2% -> 3% of each run, Pallas kernels for 0% -> 0%
where the time goes in v1:
time: 352 us; the launch traced here: 350 us
  other arithmetic  117 us (33%)
  starting transfers between devices  102 us (29%)
  waiting for transfers between devices  58.6 us (17%)
  local copies, waits for them, and re-layouts  49 us (14%)
  between operations  16.7 us (5%)
  matrix products  7.1 us (2%)
    ppermute x11, starting transfers between devices, extended(): lax.ppermute(lax.slice_in_dim(block, block.shape[dim] - width, None, axis...  58.3 us
    add x3, other arithmetic, combine(): total = total + coef[:, index, None, None] * vectors[index]  37.6 us
    reduce_sum x3, other arithmetic, inner_table(): jnp.sum(vectors[first] * vectors[second], axis=(1, 2))  30.4 us
    ppermute x8, starting transfers between devices, shards(): lax.ppermute(result, 'tile', [(i_2, i_2 ^ far) for i_2 in range(count_2)])  29.4 us
    unnamed x162, local copies, waits for them, and re-layouts  23.1 us
    ppermute x11, waiting for transfers between devices, extended(): lax.ppermute(lax.slice_in_dim(block, block.shape[dim] - width, None, axis...  16.7 us
    reduce_scatter x1, waiting for transfers between devices, shards(): lax.psum_scatter(jnp.dot(own_cols, flat, preferred_element_type=jnp.float...  15.9 us
    ppermute x8, waiting for transfers between devices, shards(): lax.ppermute(result, 'tile', [(i_2, i_2 ^ far) for i_2 in range(count_2)])  14.6 us
  transfers between devices with their start and end apart: 31, of which 22 were waited for; matrix products, arithmetic and copies ran while one was open for 3% of the time, Pallas kernels for 0%

profile of v1, /device:TPU:0, one launch (start us, length us, event | category | flops | bytes accessed | tf_op | source)
XLA Modules:
  0.0 349.9 jit_solution(12589210711471095633)
XLA Ops:
  12.1 4.9 %fusion.44 = f32[80,16384]{1,0:T(8,128)} fusion(bf16[68,16384]{1,0:T(8,128)(2,1)} %bitcast.230, bf16[80,136]{0,1:T(8,128)(2,1)S(1)} %copy-done, s32[]{:T(128)S(6)} %select_n.3), kind=kOutput, calls=%fused_computation.212 | convolution fusion | flops 178257920 | bytes 7489540 | tf_op jit(solution)/shard_map/dot_general | solution.py:74
  17.0 15.9 %reduce-scatter.2.cloned.1.call-done = f32[40,16384]{1,0:T(8,128)} async-done(((f32[80,16384]{1,0:T(8,128)}), f32[40,16384]{1,0:T(8,128)}) %reduce-scatter.2.cloned.1.call-update) | async-done | bytes 2621456 | tf_op jit(solution)/shard_map/reduce_scatter | solution.py:73
  36.3 4.6 %collective-permute-start.1 = (f32[40,1,1024]{2,0,1:T(8,128)S(1)}, f32[40,1,1024]{2,0,1:T(8,128)S(1)}, u32[]{:S(2)}, u32[]{:S(2)}) collective-permute-start(f32[40,1,1024]{2,0,1:T(8,128)S(1)} %get-tuple-element.133), channel_id=1, source_target_pairs={{0,2},{2,4},{4,6},{6,8},{8,10},{10,12},{12,14},{14,16},{16,18},{18... | collective-permute-start | bytes 491528 | tf_op jit(solution)/shard_map/ppermute | solution.py:17
  43.3 4.5 %collective-permute-done.1 = f32[40,1,1024]{2,0,1:T(8,128)S(1)} collective-permute-done((f32[40,1,1024]{2,0,1:T(8,128)S(1)}, f32[40,1,1024]{2,0,1:T(8,128)S(1)}, u32[]{:S(2)}, u32[]{:S(2)}) %collective-permute-start.1) | collective-permute-done | bytes 163872 | tf_op jit(solution)/shard_map/ppermute | solution.py:17
  50.6 5.0 %collective-permute-start.3 = (f32[40,1,1024]{2,0,1:T(8,128)S(1)}, f32[40,1,1024]{2,0,1:T(8,128)S(1)}, u32[]{:S(2)}, u32[]{:S(2)}) collective-permute-start(f32[40,1,1024]{2,0,1:T(8,128)S(1)} %get-tuple-element.131), channel_id=1, source_target_pairs={{0,2},{2,4},{4,6},{6,8},{8,10},{10,12},{12,14},{14,16},{16,18},{18... | collective-permute-start | bytes 491528 | tf_op jit(solution)/shard_map/ppermute | solution.py:17
  62.9 5.3 %collective-permute-start.5 = (f32[40,1,1024]{2,0,1:T(8,128)S(1)}, f32[40,1,1024]{2,0,1:T(8,128)S(1)}, u32[]{:S(2)}, u32[]{:S(2)}) collective-permute-start(f32[40,1,1024]{2,0,1:T(8,128)S(1)} %get-tuple-element.129), channel_id=1, source_target_pairs={{0,2},{2,4},{4,6},{6,8},{8,10},{10,12},{12,14},{14,16},{16,18},{18... | collective-permute-start | bytes 491528 | tf_op jit(solution)/shard_map/ppermute | solution.py:17
  77.6 5.2 %collective-permute-start.7 = (f32[40,1,1024]{2,0,1:T(8,128)S(1)}, f32[40,1,1024]{2,0,1:T(8,128)S(1)}, u32[]{:S(2)}, u32[]{:S(2)}) collective-permute-start(f32[40,1,1024]{2,0,1:T(8,128)S(1)} %get-tuple-element.127), channel_id=1, source_target_pairs={{0,2},{2,4},{4,6},{6,8},{8,10},{10,12},{12,14},{14,16},{16,18},{18... | collective-permute-start | bytes 491528 | tf_op jit(solution)/shard_map/ppermute | solution.py:17
  87.5 5.4 %multiply_reduce_fusion.45 = (f32[40]{0:T(128)S(1)}, f32[40]{0:T(128)S(1)}, f32[40]{0:T(128)S(1)}, f32[40]{0:T(128)S(1)}, f32[40]{0:T(128)S(1)}, /*index=5*/f32[...) fusion(f32[40,16,1024]{2,0,1:T(8,128)S(1)} %fusion.8, ...), kind=kLoop, calls=%fused_computation.138 | loop fusion | flops 26213840 | bytes 11143520 | tf_op jit(solution)/shard_map/reduce_sum | solution.py:58
  118.8 13.7 %multiply_add_fusion.2 = f32[40,16,1024]{2,0,1:T(8,128)S(1)} fusion(f32[40,16,1024]{2,0,1:T(8,128)} %copy-done.6, f32[40,16,1024]{2,0,1:T(8,128)} %get-tuple-element.111, f32[40]{0:T(128)S(1)} %get-tuple-element.164, f32[40]{0:T(128)S(1)} %get-tuple-element.165, f32[40]{0:T(128)S(1)} %get-tuple-element.166, f32[40]{0:T(128)S(1)} %get-tuple-element.167, ...), kind=kLoop, calls=%fused_computation.137 | loop fusion | flops 19005440 | bytes 13764160 | tf_op jit(solution)/shard_map/add | solution.py:49
  133.8 4.6 %collective-permute-start.13 = (f32[40,1,1024]{2,0,1:T(8,128)S(1)}, f32[40,1,1024]{2,0,1:T(8,128)S(1)}, u32[]{:S(2)}, u32[]{:S(2)}) collective-permute-start(f32[40,1,1024]{2,0,1:T(8,128)S(1)} %get-tuple-element.121), channel_id=1, source_target_pairs={{0,2},{2,4},{4,6},{6,8},{8,10},{10,12},{12,14},{14,16},{16,18},{18... | collective-permute-start | bytes 491528 | tf_op jit(solution)/shard_map/ppermute | solution.py:17
  138.4 4.8 %multiply_add_fusion.1 = f32[40,16,1024]{2,0,1:T(8,128)S(1)} fusion(f32[40,16,1024]{2,0,1:T(8,128)S(1)} %copy-done.7, f32[40,16,1024]{2,0,1:T(8,128)S(1)} %copy-done.17, f32[40]{0:T(128)S(1)} %get-tuple-element.173, f32[40]{0:T(128)S(1)} %get-tuple-element.174, f32[40]{0:T(128)S(1)} %get-tuple-element.175, f32[40]{0:T(128)S(1)} %get-tuple-element.176, ...), kind=kLoop, calls=%fused_computation.131 | loop fusion | flops 19005440 | bytes 13764160 | tf_op jit(solution)/shard_map/add | solution.py:49
  146.0 4.7 %collective-permute-start.15 = (f32[40,1,1024]{2,0,1:T(8,128)S(1)}, f32[40,1,1024]{2,0,1:T(8,128)S(1)}, u32[]{:S(2)}, u32[]{:S(2)}) collective-permute-start(f32[40,1,1024]{2,0,1:T(8,128)S(1)} %get-tuple-element.119), channel_id=1, source_target_pairs={{0,2},{2,4},{4,6},{6,8},{8,10},{10,12},{12,14},{14,16},{16,18},{18... | collective-permute-start | bytes 491528 | tf_op jit(solution)/shard_map/ppermute | solution.py:17
  152.0 5.4 %collective-permute-start.21 = (f32[40,1,1024]{2,0,1:T(8,128)S(1)}, f32[40,1,1024]{2,0,1:T(8,128)S(1)}, u32[]{:S(2)}, u32[]{:S(2)}) collective-permute-start(f32[40,1,1024]{2,0,1:T(8,128)S(1)} %get-tuple-element.125), channel_id=1, source_target_pairs={{0,2},{2,4},{4,6},{6,8},{8,10},{10,12},{12,14},{14,16},{16,18},{18... | collective-permute-start | bytes 491528 | tf_op jit(solution)/shard_map/ppermute | solution.py:17
  160.9 5.0 %collective-permute-start.17 = (f32[40,1,1024]{2,0,1:T(8,128)S(1)}, f32[40,1,1024]{2,0,1:T(8,128)S(1)}, u32[]{:S(2)}, u32[]{:S(2)}) collective-permute-start(f32[40,1,1024]{2,0,1:T(8,128)S(1)} %get-tuple-element.117), channel_id=1, source_target_pairs={{0,2},{2,4},{4,6},{6,8},{8,10},{10,12},{12,14},{14,16},{16,18},{18... | collective-permute-start | bytes 491528 | tf_op jit(solution)/shard_map/ppermute | solution.py:17
  173.4 5.5 %collective-permute-start.23 = (f32[40,1,1024]{2,0,1:T(8,128)S(1)}, f32[40,1,1024]{2,0,1:T(8,128)S(1)}, u32[]{:S(2)}, u32[]{:S(2)}) collective-permute-start(f32[40,1,1024]{2,0,1:T(8,128)S(1)} %get-tuple-element.123), channel_id=1, source_target_pairs={{0,2},{2,4},{4,6},{6,8},{8,10},{10,12},{12,14},{14,16},{16,18},{18... | collective-permute-start | bytes 491528 | tf_op jit(solution)/shard_map/ppermute | solution.py:17
  180.1 6.6 %collective-permute-start.19 = (f32[40,1,1024]{2,0,1:T(8,128)S(1)}, f32[40,1,1024]{2,0,1:T(8,128)}, u32[]{:S(2)}, u32[]{:S(2)}) collective-permute-start(f32[40,1,1024]{2,0,1:T(8,128)S(1)} %get-tuple-element.115), channel_id=1, source_target_pairs={{0,2},{2,4},{4,6},{6,8},{8,10},{10,12},{12,14},{14,16},{16,18},{18... | collective-permute-start | bytes 491528 | tf_op jit(solution)/shard_map/ppermute | solution.py:17
  191.0 6.4 %collective-permute-start.25 = (f32[40,1,1024]{2,0,1:T(8,128)S(1)}, f32[40,1,1024]{2,0,1:T(8,128)}, u32[]{:S(2)}, u32[]{:S(2)}) collective-permute-start(f32[40,1,1024]{2,0,1:T(8,128)S(1)} %get-tuple-element.113), channel_id=1, source_target_pairs={{0,2},{2,4},{4,6},{6,8},{8,10},{10,12},{12,14},{14,16},{16,18},{18... | collective-permute-start | bytes 491528 | tf_op jit(solution)/shard_map/ppermute | solution.py:17
  199.6 24.7 %multiply_reduce_fusion = (f32[40]{0:T(128)}, f32[40]{0:T(128)}, f32[40]{0:T(128)}, f32[40]{0:T(128)}, f32[40]{0:T(128)}, /*index=5*/f32[40]{0:T(128)}, f32[40]{...) fusion(f32[40,16,1024]{2,0,1:T(8,128)} %copy-done.18, ...), kind=kLoop, calls=%fused_computation.91 | loop fusion | flops 70777080 | bytes 21961920 | tf_op jit(solution)/shard_map/reduce_sum | solution.py:58
  236.9 4.4 %collective-permute-start.26 = (f32[40,9,9]{0,2,1:T(8,128)S(1)}, f32[40,9,9]{0,2,1:T(8,128)S(1)}, u32[]{:S(2)}, u32[]{:S(2)}) collective-permute-start(f32[40,9,9]{0,2,1:T(8,128)S(1)} %constant_dynamic-update-slice_fusion.9), channel_id=1, source_target_pairs={{0,2},{2,0},{4,6},{6,4},{8,10},{10,8},{12,14},{14,12},{16,18},{18,... | collective-permute-start | bytes 38888 | tf_op jit(solution)/shard_map/ppermute | solution.py:101
  243.7 6.2 %collective-permute-start.27 = (f32[40,9,9]{0,2,1:T(8,128)S(1)}, f32[40,9,9]{0,2,1:T(8,128)S(1)}, u32[]{:S(2)}, u32[]{:S(2)}) collective-permute-start(f32[40,9,9]{0,2,1:T(8,128)S(1)} %add.408), channel_id=1, source_target_pairs={{0,4},{2,6},{4,0},{6,2},{8,12},{10,14},{12,8},{14,10},{16,20},{18,... | collective-permute-start | bytes 38888 | tf_op jit(solution)/shard_map/ppermute | solution.py:101
  252.3 5.6 %collective-permute-start.28 = (f32[40,9,9]{0,2,1:T(8,128)S(1)}, f32[40,9,9]{0,2,1:T(8,128)S(1)}, u32[]{:S(2)}, u32[]{:S(2)}) collective-permute-start(f32[40,9,9]{0,2,1:T(8,128)S(1)} %add.409), channel_id=1, source_target_pairs={{0,8},{2,10},{4,12},{6,14},{8,0},{10,2},{12,4},{14,6},{16,24},{18,... | collective-permute-start | bytes 38888 | tf_op jit(solution)/shard_map/ppermute | solution.py:101
  303.0 19.2 %multiply_add_fusion = f32[40,16,1024]{2,0,1:T(8,128)} fusion(f32[40,16,1024]{2,0,1:T(8,128)} %get-tuple-element.109, f32[40,16,1024]{2,0,1:T(8,128)} %copy-done.15, f32[40,16,1024]{2,0,1:T(8,128)} %copy-done.11, f32[40,16,1024]{2,0,1:T(8,128)} %get-tuple-element.108, f32[40,16,1024]{2,0,1:T(8,128)} %copy-done.16, f32[40,16,1024]{2,0,1:T(8,128)} %copy-done.13, ...), kind=kLoop, calls=%fused_computation.89 | loop fusion | flops 19005440 | bytes 21628480 | tf_op jit(solution)/shard_map/add | solution.py:49
  322.3 4.9 %copy.22 = f32[40,16,1024]{2,1,0:T(8,128)} copy(f32[40,16,1024]{2,0,1:T(8,128)} %multiply_add_fusion) | data formatting | bytes 5242880
  327.3 12.7 %add_add_fusion = f32[40,16,1024]{2,0,1:T(8,128)S(1)} fusion(f32[40,16,1024]{2,0,1:T(8,128)} %get-tuple-element.109, f32[40,16,1024]{2,0,1:T(8,128)} %copy-done.15, f32[40,16,1024]{2,0,1:T(8,128)S(1)} %copy-done.12, f32[40,16,1024]{2,0,1:T(8,128)} %get-tuple-element.108, f32[40,16,1024]{2,0,1:T(8,128)} %copy-done.16, f32[40,16,1024]{2,0,1:T(8,128)S(1)} %copy-done.14, ...), kind=kLoop, calls=%fused_computation.90 | loop fusion | flops 38666240 | bytes 32771040 | tf_op jit(solution)/shard_map/add | solution.py:118
  (345 shorter events, 148.0 us)
Async XLA Ops:
  7.2 25.7 %reduce-scatter.2.cloned.1.call-start = ((), (), s32[]{:S(2)}) async-start(), calls=%async_computation.1 | async-start | bytes 7864320 | tf_op jit(solution)/shard_map/reduce_scatter | solution.py:73
  35.0 8.3 %collective-permute-start = (f32[40,1,1024]{2,0,1:T(8,128)S(1)}, f32[40,1,1024]{2,0,1:T(8,128)S(1)}, u32[]{:S(2)}, u32[]{:S(2)}) collective-permute-start(f32[40,1,1024]{2,0,1:T(8,128)S(1)} %get-tuple-element.132), channel_id=1, source_target_pairs={{2,0},{4,2},{6,4},{8,6},{10,8},{12,10},{14,12},{16,14},{18,16},{20... | collective-permute-start | bytes 491528 | tf_op jit(solution)/shard_map/ppermute | solution.py:20
  36.3 11.5 %collective-permute-start.1 = (f32[40,1,1024]{2,0,1:T(8,128)S(1)}, f32[40,1,1024]{2,0,1:T(8,128)S(1)}, u32[]{:S(2)}, u32[]{:S(2)}) collective-permute-start(f32[40,1,1024]{2,0,1:T(8,128)S(1)} %get-tuple-element.133), channel_id=1, source_target_pairs={{0,2},{2,4},{4,6},{6,8},{8,10},{10,12},{12,14},{14,16},{16,18},{18... | collective-permute-start | bytes 491528 | tf_op jit(solution)/shard_map/ppermute | solution.py:17
  49.3 8.8 %collective-permute-start.2 = (f32[40,1,1024]{2,0,1:T(8,128)S(1)}, f32[40,1,1024]{2,0,1:T(8,128)S(1)}, u32[]{:S(2)}, u32[]{:S(2)}) collective-permute-start(f32[40,1,1024]{2,0,1:T(8,128)S(1)} %get-tuple-element.130), channel_id=1, source_target_pairs={{2,0},{4,2},{6,4},{8,6},{10,8},{12,10},{14,12},{16,14},{18,16},{20... | collective-permute-start | bytes 491528 | tf_op jit(solution)/shard_map/ppermute | solution.py:20
  50.6 9.5 %collective-permute-start.3 = (f32[40,1,1024]{2,0,1:T(8,128)S(1)}, f32[40,1,1024]{2,0,1:T(8,128)S(1)}, u32[]{:S(2)}, u32[]{:S(2)}) collective-permute-start(f32[40,1,1024]{2,0,1:T(8,128)S(1)} %get-tuple-element.131), channel_id=1, source_target_pairs={{0,2},{2,4},{4,6},{6,8},{8,10},{10,12},{12,14},{14,16},{16,18},{18... | collective-permute-start | bytes 491528 | tf_op jit(solution)/shard_map/ppermute | solution.py:17
  61.6 8.8 %collective-permute-start.4 = (f32[40,1,1024]{2,0,1:T(8,128)S(1)}, f32[40,1,1024]{2,0,1:T(8,128)S(1)}, u32[]{:S(2)}, u32[]{:S(2)}) collective-permute-start(f32[40,1,1024]{2,0,1:T(8,128)S(1)} %get-tuple-element.128), channel_id=1, source_target_pairs={{2,0},{4,2},{6,4},{8,6},{10,8},{12,10},{14,12},{16,14},{18,16},{20... | collective-permute-start | bytes 491528 | tf_op jit(solution)/shard_map/ppermute | solution.py:20
  62.9 11.9 %collective-permute-start.5 = (f32[40,1,1024]{2,0,1:T(8,128)S(1)}, f32[40,1,1024]{2,0,1:T(8,128)S(1)}, u32[]{:S(2)}, u32[]{:S(2)}) collective-permute-start(f32[40,1,1024]{2,0,1:T(8,128)S(1)} %get-tuple-element.129), channel_id=1, source_target_pairs={{0,2},{2,4},{4,6},{6,8},{8,10},{10,12},{12,14},{14,16},{16,18},{18... | collective-permute-start | bytes 491528 | tf_op jit(solution)/shard_map/ppermute | solution.py:17
  76.3 8.8 %collective-permute-start.6 = (f32[40,1,1024]{2,0,1:T(8,128)S(1)}, f32[40,1,1024]{2,0,1:T(8,128)S(1)}, u32[]{:S(2)}, u32[]{:S(2)}) collective-permute-start(f32[40,1,1024]{2,0,1:T(8,128)S(1)} %get-tuple-element.126), channel_id=1, source_target_pairs={{2,0},{4,2},{6,4},{8,6},{10,8},{12,10},{14,12},{16,14},{18,16},{20... | collective-permute-start | bytes 491528 | tf_op jit(solution)/shard_map/ppermute | solution.py:20
  77.6 10.0 %collective-permute-start.7 = (f32[40,1,1024]{2,0,1:T(8,128)S(1)}, f32[40,1,1024]{2,0,1:T(8,128)S(1)}, u32[]{:S(2)}, u32[]{:S(2)}) collective-permute-start(f32[40,1,1024]{2,0,1:T(8,128)S(1)} %get-tuple-element.127), channel_id=1, source_target_pairs={{0,2},{2,4},{4,6},{6,8},{8,10},{10,12},{12,14},{14,16},{16,18},{18... | collective-permute-start | bytes 491528 | tf_op jit(solution)/shard_map/ppermute | solution.py:17
  132.5 10.7 %collective-permute-start.12 = (f32[40,1,1024]{2,0,1:T(8,128)S(1)}, f32[40,1,1024]{2,0,1:T(8,128)S(1)}, u32[]{:S(2)}, u32[]{:S(2)}) collective-permute-start(f32[40,1,1024]{2,0,1:T(8,128)S(1)} %get-tuple-element.120), channel_id=1, source_target_pairs={{2,0},{4,2},{6,4},{8,6},{10,8},{12,10},{14,12},{16,14},{18,16},{20... | collective-permute-start | bytes 491528 | tf_op jit(solution)/shard_map/ppermute | solution.py:20
  133.8 9.4 %collective-permute-start.13 = (f32[40,1,1024]{2,0,1:T(8,128)S(1)}, f32[40,1,1024]{2,0,1:T(8,128)S(1)}, u32[]{:S(2)}, u32[]{:S(2)}) collective-permute-start(f32[40,1,1024]{2,0,1:T(8,128)S(1)} %get-tuple-element.121), channel_id=1, source_target_pairs={{0,2},{2,4},{4,6},{6,8},{8,10},{10,12},{12,14},{14,16},{16,18},{18... | collective-permute-start | bytes 491528 | tf_op jit(solution)/shard_map/ppermute | solution.py:17
  144.7 12.8 %collective-permute-start.14 = (f32[40,1,1024]{2,0,1:T(8,128)S(1)}, f32[40,1,1024]{2,0,1:T(8,128)S(1)}, u32[]{:S(2)}, u32[]{:S(2)}) collective-permute-start(f32[40,1,1024]{2,0,1:T(8,128)S(1)} %get-tuple-element.118), channel_id=1, source_target_pairs={{2,0},{4,2},{6,4},{8,6},{10,8},{12,10},{14,12},{16,14},{18,16},{20... | collective-permute-start | bytes 491528 | tf_op jit(solution)/shard_map/ppermute | solution.py:20
  146.0 12.1 %collective-permute-start.15 = (f32[40,1,1024]{2,0,1:T(8,128)S(1)}, f32[40,1,1024]{2,0,1:T(8,128)S(1)}, u32[]{:S(2)}, u32[]{:S(2)}) collective-permute-start(f32[40,1,1024]{2,0,1:T(8,128)S(1)} %get-tuple-element.119), channel_id=1, source_target_pairs={{0,2},{2,4},{4,6},{6,8},{8,10},{10,12},{12,14},{14,16},{16,18},{18... | collective-permute-start | bytes 491528 | tf_op jit(solution)/shard_map/ppermute | solution.py:17
  150.7 15.2 %collective-permute-start.20 = (f32[40,1,1024]{2,0,1:T(8,128)S(1)}, f32[40,1,1024]{2,0,1:T(8,128)S(1)}, u32[]{:S(2)}, u32[]{:S(2)}) collective-permute-start(f32[40,1,1024]{2,0,1:T(8,128)S(1)} %get-tuple-element.124), channel_id=1, source_target_pairs={{2,0},{4,2},{6,4},{8,6},{10,8},{12,10},{14,12},{16,14},{18,16},{20... | collective-permute-start | bytes 491528 | tf_op jit(solution)/shard_map/ppermute | solution.py:20
  152.0 13.9 %collective-permute-start.21 = (f32[40,1,1024]{2,0,1:T(8,128)S(1)}, f32[40,1,1024]{2,0,1:T(8,128)S(1)}, u32[]{:S(2)}, u32[]{:S(2)}) collective-permute-start(f32[40,1,1024]{2,0,1:T(8,128)S(1)} %get-tuple-element.125), channel_id=1, source_target_pairs={{0,2},{2,4},{4,6},{6,8},{8,10},{10,12},{12,14},{14,16},{16,18},{18... | collective-permute-start | bytes 491528 | tf_op jit(solution)/shard_map/ppermute | solution.py:17
  159.6 7.9 %collective-permute-start.16 = (f32[40,1,1024]{2,0,1:T(8,128)S(1)}, f32[40,1,1024]{2,0,1:T(8,128)S(1)}, u32[]{:S(2)}, u32[]{:S(2)}) collective-permute-start(f32[40,1,1024]{2,0,1:T(8,128)S(1)} %get-tuple-element.116), channel_id=1, source_target_pairs={{2,0},{4,2},{6,4},{8,6},{10,8},{12,10},{14,12},{16,14},{18,16},{20... | collective-permute-start | bytes 491528 | tf_op jit(solution)/shard_map/ppermute | solution.py:20
  172.1 14.7 %collective-permute-start.22 = (f32[40,1,1024]{2,0,1:T(8,128)S(1)}, f32[40,1,1024]{2,0,1:T(8,128)S(1)}, u32[]{:S(2)}, u32[]{:S(2)}) collective-permute-start(f32[40,1,1024]{2,0,1:T(8,128)S(1)} %get-tuple-element.122), channel_id=1, source_target_pairs={{2,0},{4,2},{6,4},{8,6},{10,8},{12,10},{14,12},{16,14},{18,16},{20... | collective-permute-start | bytes 491528 | tf_op jit(solution)/shard_map/ppermute | solution.py:20
  173.4 13.4 %collective-permute-start.23 = (f32[40,1,1024]{2,0,1:T(8,128)S(1)}, f32[40,1,1024]{2,0,1:T(8,128)S(1)}, u32[]{:S(2)}, u32[]{:S(2)}) collective-permute-start(f32[40,1,1024]{2,0,1:T(8,128)S(1)} %get-tuple-element.123), channel_id=1, source_target_pairs={{0,2},{2,4},{4,6},{6,8},{8,10},{10,12},{12,14},{14,16},{16,18},{18... | collective-permute-start | bytes 491528 | tf_op jit(solution)/shard_map/ppermute | solution.py:17
  178.8 18.6 %collective-permute-start.18 = (f32[40,1,1024]{2,0,1:T(8,128)S(1)}, f32[40,1,1024]{2,0,1:T(8,128)}, u32[]{:S(2)}, u32[]{:S(2)}) collective-permute-start(f32[40,1,1024]{2,0,1:T(8,128)S(1)} %get-tuple-element.114), channel_id=1, source_target_pairs={{2,0},{4,2},{6,4},{8,6},{10,8},{12,10},{14,12},{16,14},{18,16},{20... | collective-permute-start | bytes 491528 | tf_op jit(solution)/shard_map/ppermute | solution.py:20
  180.1 17.3 %collective-permute-start.19 = (f32[40,1,1024]{2,0,1:T(8,128)S(1)}, f32[40,1,1024]{2,0,1:T(8,128)}, u32[]{:S(2)}, u32[]{:S(2)}) collective-permute-start(f32[40,1,1024]{2,0,1:T(8,128)S(1)} %get-tuple-element.115), channel_id=1, source_target_pairs={{0,2},{2,4},{4,6},{6,8},{8,10},{10,12},{12,14},{14,16},{16,18},{18... | collective-permute-start | bytes 491528 | tf_op jit(solution)/shard_map/ppermute | solution.py:17
  189.7 8.5 %collective-permute-start.24 = (f32[40,1,1024]{2,0,1:T(8,128)S(1)}, f32[40,1,1024]{2,0,1:T(8,128)}, u32[]{:S(2)}, u32[]{:S(2)}) collective-permute-start(f32[40,1,1024]{2,0,1:T(8,128)S(1)} %get-tuple-element.112), channel_id=1, source_target_pairs={{2,0},{4,2},{6,4},{8,6},{10,8},{12,10},{14,12},{16,14},{18,16},{20... | collective-permute-start | bytes 491528 | tf_op jit(solution)/shard_map/ppermute | solution.py:20
  191.0 8.6 %collective-permute-start.25 = (f32[40,1,1024]{2,0,1:T(8,128)S(1)}, f32[40,1,1024]{2,0,1:T(8,128)}, u32[]{:S(2)}, u32[]{:S(2)}) collective-permute-start(f32[40,1,1024]{2,0,1:T(8,128)S(1)} %get-tuple-element.113), channel_id=1, source_target_pairs={{0,2},{2,4},{4,6},{6,8},{8,10},{10,12},{12,14},{14,16},{16,18},{18... | collective-permute-start | bytes 491528 | tf_op jit(solution)/shard_map/ppermute | solution.py:17
  243.7 8.6 %collective-permute-start.27 = (f32[40,9,9]{0,2,1:T(8,128)S(1)}, f32[40,9,9]{0,2,1:T(8,128)S(1)}, u32[]{:S(2)}, u32[]{:S(2)}) collective-permute-start(f32[40,9,9]{0,2,1:T(8,128)S(1)} %add.408), channel_id=1, source_target_pairs={{0,4},{2,6},{4,0},{6,2},{8,12},{10,14},{12,8},{14,10},{16,20},{18,... | collective-permute-start | bytes 38888 | tf_op jit(solution)/shard_map/ppermute | solution.py:101
  252.3 7.9 %collective-permute-start.28 = (f32[40,9,9]{0,2,1:T(8,128)S(1)}, f32[40,9,9]{0,2,1:T(8,128)S(1)}, u32[]{:S(2)}, u32[]{:S(2)}) collective-permute-start(f32[40,9,9]{0,2,1:T(8,128)S(1)} %add.409), channel_id=1, source_target_pairs={{0,8},{2,10},{4,12},{6,14},{8,0},{10,2},{12,4},{14,6},{16,24},{18,... | collective-permute-start | bytes 38888 | tf_op jit(solution)/shard_map/ppermute | solution.py:101
  (71 other events, 922.6 us)
Sparse Core Ops, SparseCore 0:
  17.1 15.7 reduce-scatter.1
